TPU v7x, 32 devices: a whole 2x2x4 slice. The times are simulated.
32 devices in a mesh: bank: 8 (over z, core), zero: 4 (over y, x).
Axes of the slice: x: 2, y: 2, z: 4, core: 2. Of those that a mesh axis runs over, the one named last changes fastest.
Arguments:
- w_down: float32 [64, 1024, 2048], P('bank', None, 'zero'), may hold values from -0.25 to 0.25
- avg_down: float32 [64, 1024, 2048], P('bank', None, 'zero'), may hold values from -0.1875 to 0.1875
- mix_share: float32 [64], P('bank'), may hold values from 0.2 to 0.8
- router_weight: float32 [2048, 64], P('zero', 'bank'), may hold values from -0.125 to 0.125
- router_gain: float32 [2048], P('zero'), may hold values from 0.25 to 1.75
Outputs:
- serve_down: bfloat16 [64, 1024, 2048], P('bank')
- scale_down: float32 [64, 1024], P('bank')
- serve_router: bfloat16 [2048, 64], replicated
All inputs are finite; a program needn't handle non-finite values. Where the computation divides by a largest or mean magnitude, that divisor is 1e-20 or more.
Results may differ from a plain program's by a relative error of at most 0.001.
Values may be sent and summed in bfloat16 or wider, within the bound.
A program may use at most 192 MiB of HBM per device.

v0:
```python
import jax
import jax.numpy as jnp
from jax import lax
from jax.sharding import PartitionSpec as P


def per_device(w_down, avg_down, mix_share, router_weight, router_gain):
    fresh_down = mix_share[:, None, None] * w_down + (1.0 - mix_share[:, None, None]) * avg_down
    scale_down = lax.pmax(jnp.max(jnp.abs(fresh_down), axis=2), "zero")
    narrow_down = (fresh_down / jnp.expand_dims(scale_down, 2)).astype(jnp.bfloat16)
    serve_down = lax.all_gather(narrow_down, "zero", axis=2, tiled=True)
    part_router = (router_weight * router_gain[:, None]).astype(jnp.bfloat16)
    row_router = lax.all_gather(part_router, "zero", axis=0, tiled=True)
    serve_router = lax.all_gather(row_router, "bank", axis=1, tiled=True)
    return (serve_down, scale_down, serve_router)


def solution(mesh):
    return jax.shard_map(
        per_device,
        mesh=mesh,
        in_specs=(
            P("bank", None, "zero"),
            P("bank", None, "zero"),
            P("bank"),
            P("zero", "bank"),
            P("zero"),
        ),
        out_specs=(P("bank", None, None), P("bank", None), P()),
        check_vma=False,
    )
```

profile of v0, /device:TPU:0, one launch (start us, length us, event | category | flops | bytes accessed | tf_op | source)
XLA Modules:
  0.0 380.9 jit_solution(914199774907210939)
XLA Ops:
  7.2 0.0 all-gather.2.cloned.1.call-start
  7.2 0.7 broadcast_subtract_fusion
  7.9 0.0 copy-start.3
  7.9 13.2 %abs_reduce_fusion = f32[8,1024]{1,0:T(8,128)S(1)} fusion(f32[8,1024,512]{2,1,0:T(8,128)} %param.6, f32[8]{0:T(128)S(1)} %broadcast_subtract_fusion, f32[8,1024,512]{2,1,0:T(8,128)} %param.5, f32[8]{0:T(128)} %param.7), kind=kLoop, calls=%fused_computation.1 | loop fusion | flops 20963328 | bytes 33587264 | tf_op jit(solution)/shard_map/reduce_max | solution.py:9
  21.1 17.8 %pmax.7 = f32[8,1024]{1,0:T(8,128)S(1)} all-reduce(f32[8,1024]{1,0:T(8,128)S(1)} %abs_reduce_fusion), channel_id=1, replica_groups=mesh['bank'=8,'zero'=4] {'zero'}, use_global_device_ids=true, to_apply=%region_1.0 | all-reduce | flops 8192 | bytes 65536 | tf_op jit(solution)/shard_map/pmax | solution.py:9
  38.8 0.0 copy-done.3
  38.9 0.0 copy-start
  38.9 0.0 copy-start.1
  38.9 0.0 copy-start.2
  38.9 15.1 %divide_convert_fusion = bf16[8,1024,512]{2,1,0:T(8,128)(2,1)} fusion(f32[8,1024]{1,0:T(8,128)S(1)} %pmax.7, f32[8,1024,512]{2,1,0:T(8,128)} %param.6, f32[8]{0:T(128)S(1)} %broadcast_subtract_fusion, f32[8,1024,512]{2,1,0:T(8,128)} %param.5, f32[8]{0:T(128)S(1)} %copy-done.3), kind=kLoop, calls=%fused_computation | loop fusion | flops 20971520 | bytes 41975872 | tf_op jit(solution)/shard_map/convert_element_type | solution.py:10
  54.0 0.0 copy-done
  54.0 0.0 all-gather.2.cloned.1.call-update
  54.0 0.0 copy-done.1
  54.0 0.0 copy-done.2
  54.0 7.3 %all_gather.10 = bf16[2048,8]{0,1:T(8,128)(2,1)S(1)} all-gather(bf16[512,8]{0,1:T(8,128)(2,1)S(1)} %multiply_convert_fusion), channel_id=1, replica_groups=mesh['bank'=8,'zero'=4] {'zero'}, dimensions={0}, use_global_device_ids=true | all-gather | bytes 40960 | tf_op jit(solution)/shard_map/all_gather | solution.py:13
  61.3 14.4 %all_gather.11 = bf16[2048,64]{0,1:T(8,128)(2,1)S(1)} all-gather(bf16[2048,8]{0,1:T(8,128)(2,1)S(1)} %all_gather.10), channel_id=1, replica_groups=mesh['bank'=8,'zero'=4] {'bank'}, dimensions={1}, use_global_device_ids=true | all-gather | bytes 294912 | tf_op jit(solution)/shard_map/all_gather | solution.py:14
  75.7 274.8 %all-gather.2.cloned.1.call-done = bf16[8,1024,2048]{2,1,0:T(8,128)(2,1)} async-done(((bf16[8,1024,512]{2,1,0:T(8,128)(2,1)}), bf16[8,1024,2048]{2,1,0:T(8,128)(2,1)}) %all-gather.2.cloned.1.call-update) | async-done | bytes 33554448 | tf_op jit(solution)/shard_map/all_gather | solution.py:11
  350.5 22.9 %copy.10 = bf16[8,1024,2048]{2,1,0:T(8,128)(2,1)} copy(bf16[8,1024,2048]{2,1,0:T(8,128)(2,1)} %all-gather.2.cloned.1.call-done) | data formatting | bytes 67108864
  373.4 0.7 copy.11
  (1 shorter events, 0.0 us)
Async XLA Ops:
  7.2 343.3 %all-gather.2.cloned.1.call-start = ((), (), s32[]{:S(2)}) async-start(), calls=%async_computation | async-start | bytes 41943040 | tf_op jit(solution)/shard_map/all_gather | solution.py:11
  7.9 31.0 %copy-start.3 = (f32[8]{0:T(128)S(1)}, f32[8]{0:T(128)}, u32[]{:S(2)}) copy-start(f32[8]{0:T(128)} %param.7) | copy-start | bytes 100
  38.9 15.1 %copy-start = (f32[8,1024]{1,0:T(8,128)}, f32[8,1024]{1,0:T(8,128)S(1)}, u32[]{:S(2)}) copy-start(f32[8,1024]{1,0:T(8,128)S(1)} %pmax.7) | copy-start | bytes 98308
  38.9 15.1 %copy-start.1 = (f32[512,8]{0,1:T(8,128)S(1)}, f32[512,8]{0,1:T(8,128)}, u32[]{:S(2)}) copy-start(f32[512,8]{0,1:T(8,128)} %param.8) | copy-start | bytes 49156
  38.9 15.1 %copy-start.2 = (f32[512]{0:T(512)S(1)}, f32[512]{0:T(512)}, u32[]{:S(2)}) copy-start(f32[512]{0:T(512)} %param.9) | copy-start | bytes 6148
Sparse Core Ops, SparseCore 0:
  54.1 296.3 all-gather.1
where the time goes:
time: 381 us
  waiting for transfers between devices  275 us (72%)
  blocking collectives  39.5 us (10%)
  other arithmetic  28.9 us (8%)
  local copies, waits for them, and re-layouts  23.6 us (6%)
  between operations  14.1 us (4%)
    all_gather x1, waiting for transfers between devices, per_device(): serve_down = lax.all_gather(narrow_down, 'zero', axis=2, tiled=True)  275 us
    unnamed x10, local copies, waits for them, and re-layouts  23.6 us
    pmax x1, blocking collectives, per_device(): scale_down = lax.pmax(jnp.max(jnp.abs(fresh_down), axis=2), 'zero')  17.8 us
    convert_element_type x1, other arithmetic, per_device(): (fresh_down / jnp.expand_dims(scale_down, 2)).astype(jnp.bfloat16)  15.1 us
    all_gather x1, blocking collectives, per_device(): serve_router = lax.all_gather(row_router, 'bank', axis=1, tiled=True)  14.4 us
    reduce_max x1, other arithmetic, per_device(): scale_down = lax.pmax(jnp.max(jnp.abs(fresh_down), axis=2), 'zero')  13.2 us
  transfers between devices with their start and end apart: 1, of which 1 were waited for; matrix products, arithmetic and copies ran while one was open for 0% of the time, Pallas kernels for 0%

commit v1 on v0

--- a/solution.py
+++ b/solution.py
@@ -1,10 +1,367 @@
+import functools
+
 import jax
 import jax.numpy as jnp
 from jax import lax
+from jax.experimental import pallas as pl
+from jax.experimental.pallas import tpu as pltpu
 from jax.sharding import PartitionSpec as P
 
-
-def per_device(w_down, avg_down, mix_share, router_weight, router_gain):
+MESH = pl.DeviceIdType.MESH
+LANES = 128
+ROWS = 512
+TAIL_EXPERTS = 2
+IN_SLOTS = 3
+
+
+def peers_of(zero):
+    side = lax.rem(zero, 2)
+    return zero + 1 - 2 * side, lax.rem(zero + 2, 4), 3 - zero
+
+
+def exchange_kernel(
+    banks, chunks, rows, tail,
+    w_hbm, a_hbm, mix, router_t, gain,
+    full, tail_x, tail_y, scale_out, router_out,
+    w_buf, a_buf, fresh, narrow, own_max, peer_max, scales, router_buf,
+    in_sem, max_send, max_recv, send_x, send_y, send_f, recv_x, recv_y, recv_d,
+    keep_sem, tail_sem, bank_send, bank_recv, square_send, square_recv,
+):
+    zero, bank = lax.axis_index("zero"), lax.axis_index("bank")
+    square = peers_of(zero)
+    px, py, pd = square
+    per = w_hbm.shape[1] // rows
+    width = w_hbm.shape[2]
+    blocks = rows // LANES
+    groups = width // LANES
+
+    def place(c, owner):
+        cols = pl.ds(pl.multiple_of(owner * width, width), width)
+        return full.at[lax.div(c, per), pl.ds(pl.multiple_of(lax.rem(c, per) * rows, rows), rows), cols]
+
+    def loads(c):
+        slot = lax.rem(c, IN_SLOTS)
+        piece = (lax.div(c, per), pl.ds(pl.multiple_of(lax.rem(c, per) * rows, rows), rows))
+        return (
+            pltpu.make_async_copy(w_hbm.at[piece], w_buf.at[slot], in_sem.at[0, slot]),
+            pltpu.make_async_copy(a_hbm.at[piece], a_buf.at[slot], in_sem.at[1, slot]),
+        )
+
+    def start_loads(c):
+        for copy in loads(c):
+            copy.start()
+
+    def remote(src, dst, send, recv, to):
+        return pltpu.make_async_remote_copy(
+            src_ref=src, dst_ref=dst, send_sem=send, recv_sem=recv,
+            device_id={"zero": to}, device_id_type=MESH,
+        )
+
+    def max_copy(c, k):
+        return remote(own_max.at[c], peer_max.at[k, c], max_send.at[k, c], max_recv.at[k, c], square[k])
+
+    def to_x(c, owner):
+        return remote(narrow.at[c], place(c, owner), send_x.at[c], recv_x.at[c], px)
+
+    def to_y(c, owner):
+        return remote(narrow.at[c], place(c, owner), send_y.at[c], recv_y.at[c], py)
+
+    def on_x(c):
+        return (c < chunks - tail) | (lax.rem(c, 2) == 0)
+
+    def on_y(c):
+        return (c < chunks - tail) | (lax.rem(c, 2) == 1)
+
+    def keep(c):
+        return pltpu.make_async_copy(narrow.at[c], place(c, zero), keep_sem.at[c])
+
+    def mix_stage(c):
+        for copy in loads(c):
+            copy.wait()
+
+        @pl.when(c + IN_SLOTS - 1 < chunks)
+        def _():
+            start_loads(c + IN_SLOTS - 1)
+
+        slot, half = lax.rem(c, IN_SLOTS), lax.rem(c, 2)
+        share = mix[lax.div(c, per)]
+        for j in range(blocks):
+            part = pl.ds(j * LANES, LANES)
+            value = share * w_buf[slot, part, :] + (1.0 - share) * a_buf[slot, part, :]
+            fresh[half, part, :] = value
+            size = jnp.abs(value)
+            top = size[:, :LANES]
+            for g in range(1, groups):
+                top = jnp.maximum(top, size[:, g * LANES:(g + 1) * LANES])
+            own_max[c, pl.ds(j, 1), :] = jnp.max(top.T, axis=0, keepdims=True)
+        for k in range(3):
+            max_copy(c, k).start()
+
+    def send_stage(c):
+        for k in range(3):
+            max_copy(c, k).wait_recv()
+        scale = jnp.maximum(
+            jnp.maximum(own_max[c], peer_max[0, c]), jnp.maximum(peer_max[1, c], peer_max[2, c])
+        )
+        scales[c] = scale
+        inverse = 1.0 / scale
+        half = lax.rem(c, 2)
+        for j in range(blocks):
+            part = pl.ds(j * LANES, LANES)
+            column = jnp.broadcast_to(inverse[j:j + 1, :], (LANES, LANES)).T
+            for g in range(groups):
+                cols = slice(g * LANES, (g + 1) * LANES)
+                narrow[c, part, cols] = (fresh[half, part, cols] * column).astype(narrow.dtype)
+
+        @pl.when(on_x(c))
+        def _():
+            to_x(c, zero).start()
+
+        @pl.when(on_y(c))
+        def _():
+            to_y(c, zero).start()
+
+        keep(c).start()
+
+    def forward(c, do):
+        @pl.when(lax.rem(c, 2) == 0)
+        def _():
+            do(remote(place(c, px), place(c, px), send_f.at[c], recv_d.at[c], py))
+
+        @pl.when(lax.rem(c, 2) == 1)
+        def _():
+            do(remote(place(c, py), place(c, py), send_f.at[c], recv_d.at[c], px))
+
+    for c in range(IN_SLOTS - 1):
+        start_loads(c)
+    barrier = pltpu.get_barrier_semaphore()
+    others = [lax.rem(bank + k, banks) for k in range(1, banks)]
+    for to in square:
+        pl.semaphore_signal(barrier, inc=1, device_id={"zero": to}, device_id_type=MESH)
+    for to in others:
+        pl.semaphore_signal(barrier, inc=1, device_id={"bank": to}, device_id_type=MESH)
+    pl.semaphore_wait(barrier, 3 + len(others))
+
+    mix_stage(0)
+
+    def main(c, carry):
+        mix_stage(c)
+        send_stage(c - 1)
+        return carry
+
+    lax.fori_loop(1, chunks, main, 0)
+    send_stage(chunks - 1)
+
+    tails = []
+    for n in range(tail):
+        c = chunks - tail + n
+        out = tail_y if c % 2 == 0 else tail_x
+        tails.append(pltpu.make_async_copy(narrow.at[c], out.at[n // 2], tail_sem.at[n]))
+        tails[-1].start()
+
+    router_buf[zero, bank] = (router_t[...] * gain[...]).astype(router_buf.dtype)
+    bank_copies = [
+        pltpu.make_async_remote_copy(
+            src_ref=router_buf.at[zero, bank], dst_ref=router_buf.at[zero, bank],
+            send_sem=bank_send.at[k], recv_sem=bank_recv.at[k],
+            device_id={"bank": to}, device_id_type=MESH,
+        )
+        for k, to in enumerate(others)
+    ]
+    for copy in bank_copies:
+        copy.start()
+    for k in range(len(others)):
+        source = lax.rem(bank + banks - k - 1, banks)
+        pltpu.make_async_remote_copy(
+            src_ref=router_buf.at[zero, source], dst_ref=router_buf.at[zero, source],
+            send_sem=bank_send.at[k], recv_sem=bank_recv.at[k],
+            device_id={"bank": others[k]}, device_id_type=MESH,
+        ).wait_recv()
+    square_copies = [
+        remote(router_buf.at[zero], router_buf.at[zero], square_send.at[k], square_recv.at[k], square[k])
+        for k in range(3)
+    ]
+    for copy in square_copies:
+        copy.start()
+
+    def relay(c, carry):
+        @pl.when(lax.rem(c, 2) == 0)
+        def _():
+            to_x(c, px).wait_recv()
+
+        @pl.when(lax.rem(c, 2) == 1)
+        def _():
+            to_y(c, py).wait_recv()
+
+        forward(c, lambda copy: copy.start())
+        return carry
+
+    lax.fori_loop(0, chunks, relay, 0)
+
+    for c in range(chunks):
+        scale_out[c // per:c // per + 1, pl.ds((c % per) * rows, rows)] = jnp.concatenate(
+            [scales[c, j:j + 1, :] for j in range(blocks)], axis=1
+        )
+
+    def settle(c, carry):
+        @pl.when((lax.rem(c, 2) == 1) & (c < chunks - tail))
+        def _():
+            to_x(c, px).wait_recv()
+
+        @pl.when((lax.rem(c, 2) == 0) & (c < chunks - tail))
+        def _():
+            to_y(c, py).wait_recv()
+
+        @pl.when(on_x(c))
+        def _():
+            to_x(c, zero).wait_send()
+
+        @pl.when(on_y(c))
+        def _():
+            to_y(c, zero).wait_send()
+
+        keep(c).wait()
+        for k in range(3):
+            max_copy(c, k).wait_send()
+        return carry
+
+    lax.fori_loop(0, chunks, settle, 0)
+    for copy in tails:
+        copy.wait()
+    for copy in bank_copies:
+        copy.wait_send()
+    for k in range(3):
+        square_copies[k].wait_send()
+        remote(router_buf.at[square[k]], router_buf.at[square[k]], square_send.at[k], square_recv.at[k], square[k]).wait_recv()
+    high = router_t.shape[0]
+    for z in range(4):
+        for b in range(banks):
+            router_out[b * high:(b + 1) * high, z * gain.shape[1]:(z + 1) * gain.shape[1]] = router_buf[z, b]
+
+    def last(c, carry):
+        forward(c, lambda copy: copy.wait_send())
+        remote(narrow.at[c], place(c, pd), send_f.at[c], recv_d.at[c], pd).wait_recv()
+        return carry
+
+    lax.fori_loop(0, chunks, last, 0)
+
+
+def take_kernel(full, scale, router, full_out, scale_out, router_out):
+    full_out[...] = full[...]
+    scale_out[...] = scale[...]
+    router_out[...] = router[...]
+
+
+def patch_kernel(chunks, rows, tail, from_x, from_y, base, out, x_buf, y_buf, in_sem, out_sem):
+    del base
+    zero = lax.axis_index("zero")
+    px, py, _ = peers_of(zero)
+    per, width = out.shape[1] // rows, from_x.shape[2]
+    load = [
+        pltpu.make_async_copy(src, dst, in_sem.at[k])
+        for k, (src, dst) in enumerate(((from_x, x_buf), (from_y, y_buf)))
+    ]
+    for copy in load:
+        copy.start()
+    for copy in load:
+        copy.wait()
+    stores = []
+    for n in range(tail):
+        c = chunks - tail + n
+        buf, owner = (y_buf, py) if c % 2 == 0 else (x_buf, px)
+        cols = pl.ds(pl.multiple_of(owner * width, width), width)
+        dst = out.at[c // per, pl.ds((c % per) * rows, rows), cols]
+        stores.append(pltpu.make_async_copy(buf.at[n // 2], dst, out_sem.at[n]))
+        stores[-1].start()
+    for copy in stores:
+        copy.wait()
+
+
+def on_square(banks, w_down, avg_down, mix_share, router_weight, router_gain):
+    experts, inner, width = w_down.shape
+    rows = ROWS
+    chunks = experts * inner // rows
+    tail = TAIL_EXPERTS * inner // rows
+    kind = jnp.bfloat16
+    columns, deep = router_weight.shape[1], router_weight.shape[0]
+    any_spec = pl.BlockSpec(memory_space=pl.ANY)
+    hbm_spec = pl.BlockSpec(memory_space=pltpu.HBM)
+    vmem_spec = pl.BlockSpec(memory_space=pltpu.VMEM)
+    dma = pltpu.SemaphoreType.DMA
+    half_tail = (max(tail // 2, 1), rows, width)
+    full, tail_x, tail_y, scale, router = pl.pallas_call(
+        functools.partial(exchange_kernel, banks, chunks, rows, tail),
+        out_shape=(
+            jax.ShapeDtypeStruct((experts, inner, 4 * width), kind),
+            jax.ShapeDtypeStruct(half_tail, kind),
+            jax.ShapeDtypeStruct(half_tail, kind),
+            jax.ShapeDtypeStruct((experts, inner), jnp.float32),
+            jax.ShapeDtypeStruct((columns * banks, deep * 4), kind),
+        ),
+        in_specs=[any_spec, any_spec, pl.BlockSpec(memory_space=pltpu.SMEM), vmem_spec, vmem_spec],
+        out_specs=(hbm_spec, hbm_spec, hbm_spec, vmem_spec, vmem_spec),
+        scratch_shapes=[
+            pltpu.VMEM((IN_SLOTS, rows, width), jnp.float32),
+            pltpu.VMEM((IN_SLOTS, rows, width), jnp.float32),
+            pltpu.VMEM((2, rows, width), jnp.float32),
+            pltpu.VMEM((chunks, rows, width), kind),
+            pltpu.VMEM((chunks, rows // LANES, LANES), jnp.float32),
+            pltpu.VMEM((3, chunks, rows // LANES, LANES), jnp.float32),
+            pltpu.VMEM((chunks, rows // LANES, LANES), jnp.float32),
+            pltpu.VMEM((4, banks, columns, deep), kind),
+            dma((2, IN_SLOTS)), dma((3, chunks)), dma((3, chunks)),
+            dma((chunks,)), dma((chunks,)), dma((chunks,)),
+            dma((chunks,)), dma((chunks,)), dma((chunks,)),
+            dma((chunks,)), dma((max(tail, 1),)),
+            dma((banks - 1,)), dma((banks - 1,)), dma((3,)), dma((3,)),
+        ],
+        compiler_params=pltpu.CompilerParams(
+            collective_id=0, has_side_effects=True, vmem_limit_bytes=40 * 1024 * 1024
+        ),
+        name="exchange",
+    )(w_down, avg_down, mix_share, router_weight.T, router_gain[None, :])
+
+    whole = (1, inner, 4 * width)
+    fixed = lambda e: (0, 0)
+    if tail:
+        to_x = [(z, z ^ 1) for z in range(4)]
+        to_y = [(z, z ^ 2) for z in range(4)]
+        from_x = lax.ppermute(tail_x, "zero", to_x)
+        from_y = lax.ppermute(tail_y, "zero", to_y)
+    taken, scale, router = pl.pallas_call(
+        take_kernel,
+        grid=(experts,),
+        out_shape=tuple(jax.ShapeDtypeStruct(v.shape, v.dtype) for v in (full, scale, router)),
+        in_specs=[
+            pl.BlockSpec(whole, lambda e: (e, 0, 0)),
+            pl.BlockSpec(scale.shape, fixed),
+            pl.BlockSpec(router.shape, fixed),
+        ],
+        out_specs=(
+            pl.BlockSpec(whole, lambda e: (e, 0, 0)),
+            pl.BlockSpec(scale.shape, fixed),
+            pl.BlockSpec(router.shape, fixed),
+        ),
+        cost_estimate=pl.CostEstimate(flops=0, bytes_accessed=4 * full.size, transcendentals=0),
+        name="take",
+    )(full, scale, router)
+    if tail:
+        taken = pl.pallas_call(
+            functools.partial(patch_kernel, chunks, rows, tail),
+            out_shape=jax.ShapeDtypeStruct(taken.shape, taken.dtype),
+            in_specs=[any_spec] * 3,
+            out_specs=hbm_spec,
+            scratch_shapes=[
+                pltpu.VMEM(half_tail, kind), pltpu.VMEM(half_tail, kind), dma((2,)), dma((tail,)),
+            ],
+            input_output_aliases={2: 0},
+            cost_estimate=pl.CostEstimate(flops=0, bytes_accessed=4 * from_x.size, transcendentals=0),
+            name="patch",
+        )(from_x, from_y, taken)
+    return taken, scale, router.T
+
+
+def anywhere(w_down, avg_down, mix_share, router_weight, router_gain):
     fresh_down = mix_share[:, None, None] * w_down + (1.0 - mix_share[:, None, None]) * avg_down
     scale_down = lax.pmax(jnp.max(jnp.abs(fresh_down), axis=2), "zero")
     narrow_down = (fresh_down / jnp.expand_dims(scale_down, 2)).astype(jnp.bfloat16)
@@ -16,8 +373,9 @@
 
 
 def solution(mesh):
+    body = functools.partial(on_square, mesh.shape["bank"]) if mesh.shape["zero"] == 4 else anywhere
     return jax.shard_map(
-        per_device,
+        body,
         mesh=mesh,
         in_specs=(
             P("bank", None, "zero"),

time: 381 us -> 298 us (0.78)
  Pallas kernels: 0 us -> 291 us
  waiting for transfers between devices: 275 us -> 0.01 us
  blocking collectives: 39.5 us -> 0 us
  other arithmetic: 28.9 us -> 0 us
  local copies, waits for them, and re-layouts: 23.6 us -> 4.28 us
  between operations: 14.1 us -> 0.67 us
    pallas_call x0 -> x3, Pallas kernels: none -> 291 us  [the longest x1 265 us: on_square(): pl.pallas_call(functools.partial(exchange_kernel, banks, chunks, rows, ta...]
    all_gather x1 -> x0, waiting for transfers between devices: 275 us -> none  [per_device(): serve_down = lax.all_gather(narrow_down, 'zero', axis=2, tiled=True)]
    all_gather x2 -> x0, blocking collectives: 21.7 us -> none  [the longest x1 14.4 us: per_device(): serve_router = lax.all_gather(row_router, 'bank', axis=1, tiled=True)]
    unnamed x10 -> x12, local copies, waits for them, and re-layouts: 23.6 us -> 4.28 us
    pmax x1 -> x0, blocking collectives: 17.8 us -> none  [per_device(): scale_down = lax.pmax(jnp.max(jnp.abs(fresh_down), axis=2), 'zero')]
    convert_element_type x2 -> x0, other arithmetic: 15.1 us -> none  [the longest x1 15.1 us: per_device(): (fresh_down / jnp.expand_dims(scale_down, 2)).astype(jnp.bfloat16)]
    reduce_max x1 -> x0, other arithmetic: 13.2 us -> none  [per_device(): scale_down = lax.pmax(jnp.max(jnp.abs(fresh_down), axis=2), 'zero')]
  transfers between devices with their start and end apart: 1 -> 2, of which waited for: 1 -> 0; matrix products, arithmetic and copies ran while one was open for 0% -> 0% of each run, Pallas kernels for 0% -> 8%
where the time goes in v1:
time: 298 us
  Pallas kernels  291 us (98%)
  local copies, waits for them, and re-layouts  4.28 us (1%)
    pallas_call x1, Pallas kernels, on_square(): pl.pallas_call(functools.partial(exchange_kernel, banks, chunks, rows, ta...  265 us
    pallas_call x1, Pallas kernels, on_square(): pl.pallas_call(take_kernel, grid=(experts,), out_shape=tuple((jax.ShapeDt...  22.6 us
  transfers between devices with their start and end apart: 2, of which 0 were waited for; matrix products, arithmetic and copies ran while one was open for 0% of the time, Pallas kernels for 8%

profile of v1, /device:TPU:0, one launch (start us, length us, event | category | flops | bytes accessed | tf_op | source)
XLA Modules:
  0.0 298.1 jit_solution(6426373057185182227)
XLA Ops:
  0.6 0.0 copy-start.2
  0.6 0.7 copy-done.2
  1.4 0.0 copy-start.3
  1.4 0.7 copy-done.3
  2.0 0.0 copy-start.4
  2.0 0.7 copy-done.4
  2.7 265.5 %exchange.1 = (bf16[8,1024,2048]{2,1,0:T(8,128)(2,1)}, bf16[2,512,512]{2,1,0:T(8,128)(2,1)S(1)}, bf16[2,512,512]{2,1,0:T(8,128)(2,1)S(1)}, f32[8,1024]{1,0:T(8,128)S(1)}, bf16[64,2048]{1,0:T(8,128)(2,1)S(1)}) custom-call(f32[8,1024,512]{2,1,0:T(8,128)} %w_hbm.1, f32[8,1024,512]{2,1,0:T(8,128)} %a_hbm.1, f32[8]{0:T(128)S(1)} %copy-done.4, ...), custom_call_target="tpu_custom_call" | custom-call | tf_op jit(solution)/shard_map/exchange/pallas_call | solution.py:292
  268.2 0.0 copy-start
  268.2 0.7 copy-done
  268.9 0.0 copy-start.1
  268.9 0.6 copy-done.1
  269.5 1.2 collective-permute-start
  270.7 0.9 collective-permute-start.1
  271.6 22.6 %take.1 = (bf16[8,1024,2048]{2,1,0:T(8,128)(2,1)}, f32[8,1024]{1,0:T(8,128)}, bf16[64,2048]{1,0:T(8,128)(2,1)}) custom-call(bf16[8,1024,2048]{2,1,0:T(8,128)(2,1)} %get-tuple-element.13.full, f32[8,1024]{1,0:T(8,128)} %copy-done.1, bf16[64,2048]{1,0:T(8,128)(2,1)} %copy-done), custom_call_target="tpu_custom_call" | custom-call | bytes 67108864 | tf_op jit(solution)/shard_map/take/pallas_call | solution.py:331
  294.2 0.0 collective-permute-done.from_x
  294.2 0.0 copy-start.5
  294.2 0.0 collective-permute-done.1.from_y
  294.2 0.9 copy-done.5
  295.2 2.9 patch.1
Async XLA Ops:
  0.6 0.7 copy-start.2
  1.4 0.7 copy-start.3
  2.0 0.7 copy-start.4
  268.2 0.7 copy-start
  268.9 0.6 copy-start.1
  269.5 24.8 %collective-permute-start = (bf16[2,512,512]{2,1,0:T(8,128)(2,1)S(1)}, bf16[2,512,512]{2,1,0:T(8,128)(2,1)S(1)}, u32[]{:S(2)}, u32[]{:S(2)}) collective-permute-start(bf16[2,512,512]{2,1,0:T(8,128)(2,1)S(1)} %get-tuple-element.11), channel_id=1, source_target_pairs={{0,1},{1,0},{2,3},{3,2},{4,5},{5,4},{6,7},{7,6},{8,9},{9,8},{10,11... | collective-permute-start | bytes 3145736 | tf_op jit(solution)/shard_map/ppermute | solution.py:329
  270.7 23.6 %collective-permute-start.1 = (bf16[2,512,512]{2,1,0:T(8,128)(2,1)S(1)}, bf16[2,512,512]{2,1,0:T(8,128)(2,1)}, u32[]{:S(2)}, u32[]{:S(2)}) collective-permute-start(bf16[2,512,512]{2,1,0:T(8,128)(2,1)S(1)} %get-tuple-element.12), channel_id=1, source_target_pairs={{0,2},{1,3},{2,0},{3,1},{4,6},{5,7},{6,4},{7,5},{8,10},{9,11},{10,... | collective-permute-start | bytes 3145736 | tf_op jit(solution)/shard_map/ppermute | solution.py:330
  294.2 1.0 copy-start.5

commit v2 on v1

--- a/solution.py
+++ b/solution.py
@@ -9,9 +9,12 @@
 
 MESH = pl.DeviceIdType.MESH
 LANES = 128
-ROWS = 512
+ROWS = 1024
 TAIL_EXPERTS = 2
 IN_SLOTS = 3
+HEAD = 2
+FIRST = 1
+VMEM_BYTES = 67043328
 
 
 def peers_of(zero):
@@ -21,10 +24,11 @@
 
 def exchange_kernel(
     banks, chunks, rows, tail,
-    w_hbm, a_hbm, mix, router_t, gain,
-    full, tail_x, tail_y, scale_out, router_out,
+    w_hbm, a_hbm, mix_hbm, router_hbm, gain_hbm,
+    full, tail_x, tail_y, scale_hbm, router_to,
+    mix, router_t, gain, scale_out, router_out, small_sem,
     w_buf, a_buf, fresh, narrow, own_max, peer_max, scales, router_buf,
-    in_sem, max_send, max_recv, send_x, send_y, send_f, recv_x, recv_y, recv_d,
+    in_sem, max_send, max_recv, rest_send, rest_recv, send_x, send_y, send_f, recv_x, recv_y, recv_d,
     keep_sem, tail_sem, bank_send, bank_recv, square_send, square_recv,
 ):
     zero, bank = lax.axis_index("zero"), lax.axis_index("bank")
@@ -83,35 +87,30 @@
         def _():
             start_loads(c + IN_SLOTS - 1)
 
-        slot, half = lax.rem(c, IN_SLOTS), lax.rem(c, 2)
+        slot = lax.rem(c, IN_SLOTS)
         share = mix[lax.div(c, per)]
         for j in range(blocks):
             part = pl.ds(j * LANES, LANES)
             value = share * w_buf[slot, part, :] + (1.0 - share) * a_buf[slot, part, :]
-            fresh[half, part, :] = value
+            fresh[c, part, :] = value
             size = jnp.abs(value)
             top = size[:, :LANES]
             for g in range(1, groups):
                 top = jnp.maximum(top, size[:, g * LANES:(g + 1) * LANES])
             own_max[c, pl.ds(j, 1), :] = jnp.max(top.T, axis=0, keepdims=True)
-        for k in range(3):
-            max_copy(c, k).start()
 
     def send_stage(c):
-        for k in range(3):
-            max_copy(c, k).wait_recv()
         scale = jnp.maximum(
             jnp.maximum(own_max[c], peer_max[0, c]), jnp.maximum(peer_max[1, c], peer_max[2, c])
         )
         scales[c] = scale
         inverse = 1.0 / scale
-        half = lax.rem(c, 2)
         for j in range(blocks):
             part = pl.ds(j * LANES, LANES)
             column = jnp.broadcast_to(inverse[j:j + 1, :], (LANES, LANES)).T
             for g in range(groups):
                 cols = slice(g * LANES, (g + 1) * LANES)
-                narrow[c, part, cols] = (fresh[half, part, cols] * column).astype(narrow.dtype)
+                narrow[c, part, cols] = (fresh[c, part, cols] * column).astype(narrow.dtype)
 
         @pl.when(on_x(c))
         def _():
@@ -132,8 +131,15 @@
         def _():
             do(remote(place(c, py), place(c, py), send_f.at[c], recv_d.at[c], px))
 
+    small = [
+        pltpu.make_async_copy(src, dst, small_sem.at[k])
+        for k, (src, dst) in enumerate(((mix_hbm, mix), (router_hbm, router_t), (gain_hbm, gain)))
+    ]
+    small[0].start()
     for c in range(IN_SLOTS - 1):
         start_loads(c)
+    for copy in small[1:]:
+        copy.start()
     barrier = pltpu.get_barrier_semaphore()
     others = [lax.rem(bank + k, banks) for k in range(1, banks)]
     for to in square:
@@ -142,15 +148,41 @@
         pl.semaphore_signal(barrier, inc=1, device_id={"bank": to}, device_id_type=MESH)
     pl.semaphore_wait(barrier, 3 + len(others))
 
-    mix_stage(0)
-
-    def main(c, carry):
+    small[0].wait()
+    def early(c, carry):
         mix_stage(c)
-        send_stage(c - 1)
-        return carry
-
-    lax.fori_loop(1, chunks, main, 0)
-    send_stage(chunks - 1)
+        for k in range(3):
+            max_copy(c, k).start()
+        return carry
+
+    def early_send(c, carry):
+        for k in range(3):
+            max_copy(c, k).wait_recv()
+        send_stage(c)
+        return carry
+
+    def late(c, carry):
+        mix_stage(c)
+        return carry
+
+    def late_send(c, carry):
+        send_stage(c)
+        return carry
+
+    rest = pl.ds(HEAD, chunks - HEAD)
+    rest_copies = [
+        remote(own_max.at[rest], peer_max.at[k, rest], rest_send.at[k], rest_recv.at[k], square[k])
+        for k in range(3)
+    ]
+    lax.fori_loop(0, HEAD, early, 0)
+    lax.fori_loop(0, FIRST, early_send, 0)
+    lax.fori_loop(HEAD, chunks, late, 0)
+    for copy in rest_copies:
+        copy.start()
+    lax.fori_loop(FIRST, HEAD, early_send, 0)
+    for copy in rest_copies:
+        copy.wait_recv()
+    lax.fori_loop(HEAD, chunks, late_send, 0)
 
     tails = []
     for n in range(tail):
@@ -159,6 +191,8 @@
         tails.append(pltpu.make_async_copy(narrow.at[c], out.at[n // 2], tail_sem.at[n]))
         tails[-1].start()
 
+    for copy in small[1:]:
+        copy.wait()
     router_buf[zero, bank] = (router_t[...] * gain[...]).astype(router_buf.dtype)
     bank_copies = [
         pltpu.make_async_remote_copy(
@@ -203,6 +237,9 @@
             [scales[c, j:j + 1, :] for j in range(blocks)], axis=1
         )
 
+    scale_copy = pltpu.make_async_copy(scale_out, scale_hbm, small_sem.at[3])
+    scale_copy.start()
+
     def settle(c, carry):
         @pl.when((lax.rem(c, 2) == 1) & (c < chunks - tail))
         def _():
@@ -221,11 +258,14 @@
             to_y(c, zero).wait_send()
 
         keep(c).wait()
+        return carry
+
+    lax.fori_loop(0, chunks, settle, 0)
+    for c in range(HEAD):
         for k in range(3):
             max_copy(c, k).wait_send()
-        return carry
-
-    lax.fori_loop(0, chunks, settle, 0)
+    for copy in rest_copies:
+        copy.wait_send()
     for copy in tails:
         copy.wait()
     for copy in bank_copies:
@@ -238,12 +278,17 @@
         for b in range(banks):
             router_out[b * high:(b + 1) * high, z * gain.shape[1]:(z + 1) * gain.shape[1]] = router_buf[z, b]
 
+    router_copy = pltpu.make_async_copy(router_out, router_to, small_sem.at[4])
+    router_copy.start()
+
     def last(c, carry):
         forward(c, lambda copy: copy.wait_send())
         remote(narrow.at[c], place(c, pd), send_f.at[c], recv_d.at[c], pd).wait_recv()
         return carry
 
     lax.fori_loop(0, chunks, last, 0)
+    scale_copy.wait()
+    router_copy.wait()
 
 
 def take_kernel(full, scale, router, full_out, scale_out, router_out):
@@ -252,29 +297,26 @@
     router_out[...] = router[...]
 
 
-def patch_kernel(chunks, rows, tail, from_x, from_y, base, out, x_buf, y_buf, in_sem, out_sem):
+def patch_kernel(chunks, rows, tail, from_x, from_y, base, out, buf, in_sem, out_sem):
     del base
     zero = lax.axis_index("zero")
     px, py, _ = peers_of(zero)
     per, width = out.shape[1] // rows, from_x.shape[2]
-    load = [
-        pltpu.make_async_copy(src, dst, in_sem.at[k])
-        for k, (src, dst) in enumerate(((from_x, x_buf), (from_y, y_buf)))
-    ]
-    for copy in load:
-        copy.start()
-    for copy in load:
-        copy.wait()
-    stores = []
+    loads, stores = [], []
     for n in range(tail):
         c = chunks - tail + n
-        buf, owner = (y_buf, py) if c % 2 == 0 else (x_buf, px)
+        src, owner = (from_y, py) if c % 2 == 0 else (from_x, px)
+        loads.append(pltpu.make_async_copy(src.at[n // 2], buf.at[n], in_sem.at[n]))
         cols = pl.ds(pl.multiple_of(owner * width, width), width)
         dst = out.at[c // per, pl.ds((c % per) * rows, rows), cols]
-        stores.append(pltpu.make_async_copy(buf.at[n // 2], dst, out_sem.at[n]))
-        stores[-1].start()
-    for copy in stores:
-        copy.wait()
+        stores.append(pltpu.make_async_copy(buf.at[n], dst, out_sem.at[n]))
+    for load in loads:
+        load.start()
+    for load, store in zip(loads, stores):
+        load.wait()
+        store.start()
+    for store in stores:
+        store.wait()
 
 
 def on_square(banks, w_down, avg_down, mix_share, router_weight, router_gain):
@@ -286,7 +328,6 @@
     columns, deep = router_weight.shape[1], router_weight.shape[0]
     any_spec = pl.BlockSpec(memory_space=pl.ANY)
     hbm_spec = pl.BlockSpec(memory_space=pltpu.HBM)
-    vmem_spec = pl.BlockSpec(memory_space=pltpu.VMEM)
     dma = pltpu.SemaphoreType.DMA
     half_tail = (max(tail // 2, 1), rows, width)
     full, tail_x, tail_y, scale, router = pl.pallas_call(
@@ -298,25 +339,31 @@
             jax.ShapeDtypeStruct((experts, inner), jnp.float32),
             jax.ShapeDtypeStruct((columns * banks, deep * 4), kind),
         ),
-        in_specs=[any_spec, any_spec, pl.BlockSpec(memory_space=pltpu.SMEM), vmem_spec, vmem_spec],
-        out_specs=(hbm_spec, hbm_spec, hbm_spec, vmem_spec, vmem_spec),
+        in_specs=[any_spec] * 5,
+        out_specs=(hbm_spec,) * 5,
         scratch_shapes=[
+            pltpu.SMEM(mix_share.shape, jnp.float32),
+            pltpu.VMEM((columns, deep), jnp.float32),
+            pltpu.VMEM((1, deep), jnp.float32),
+            pltpu.VMEM((experts, inner), jnp.float32),
+            pltpu.VMEM((columns * banks, deep * 4), kind),
+            dma((5,)),
             pltpu.VMEM((IN_SLOTS, rows, width), jnp.float32),
             pltpu.VMEM((IN_SLOTS, rows, width), jnp.float32),
-            pltpu.VMEM((2, rows, width), jnp.float32),
+            pltpu.VMEM((chunks, rows, width), jnp.float32),
             pltpu.VMEM((chunks, rows, width), kind),
             pltpu.VMEM((chunks, rows // LANES, LANES), jnp.float32),
             pltpu.VMEM((3, chunks, rows // LANES, LANES), jnp.float32),
             pltpu.VMEM((chunks, rows // LANES, LANES), jnp.float32),
             pltpu.VMEM((4, banks, columns, deep), kind),
-            dma((2, IN_SLOTS)), dma((3, chunks)), dma((3, chunks)),
+            dma((2, IN_SLOTS)), dma((3, HEAD)), dma((3, HEAD)), dma((3,)), dma((3,)),
             dma((chunks,)), dma((chunks,)), dma((chunks,)),
             dma((chunks,)), dma((chunks,)), dma((chunks,)),
             dma((chunks,)), dma((max(tail, 1),)),
             dma((banks - 1,)), dma((banks - 1,)), dma((3,)), dma((3,)),
         ],
         compiler_params=pltpu.CompilerParams(
-            collective_id=0, has_side_effects=True, vmem_limit_bytes=40 * 1024 * 1024
+            collective_id=0, has_side_effects=True, vmem_limit_bytes=VMEM_BYTES
         ),
         name="exchange",
     )(w_down, avg_down, mix_share, router_weight.T, router_gain[None, :])
@@ -343,6 +390,7 @@
             pl.BlockSpec(router.shape, fixed),
         ),
         cost_estimate=pl.CostEstimate(flops=0, bytes_accessed=4 * full.size, transcendentals=0),
+        compiler_params=pltpu.CompilerParams(vmem_limit_bytes=VMEM_BYTES),
         name="take",
     )(full, scale, router)
     if tail:
@@ -351,11 +399,10 @@
             out_shape=jax.ShapeDtypeStruct(taken.shape, taken.dtype),
             in_specs=[any_spec] * 3,
             out_specs=hbm_spec,
-            scratch_shapes=[
-                pltpu.VMEM(half_tail, kind), pltpu.VMEM(half_tail, kind), dma((2,)), dma((tail,)),
-            ],
+            scratch_shapes=[pltpu.VMEM((tail, rows, width), kind), dma((tail,)), dma((tail,))],
             input_output_aliases={2: 0},
             cost_estimate=pl.CostEstimate(flops=0, bytes_accessed=4 * from_x.size, transcendentals=0),
+            compiler_params=pltpu.CompilerParams(vmem_limit_bytes=VMEM_BYTES),
             name="patch",
         )(from_x, from_y, taken)
     return taken, scale, router.T

time: 298 us -> 291 us (0.977)
  local copies, waits for them, and re-layouts: 4.28 us -> 0 us
  Pallas kernels: 291 us -> 288 us
    unnamed x12 -> x0, local copies, waits for them, and re-layouts: 4.28 us -> none
  transfers between devices with their start and end apart: 2 -> 2, of which waited for: 0 -> 1; matrix products, arithmetic and copies ran while one was open for 0% -> 0% of each run, Pallas kernels for 8% -> 8%
where the time goes in v2:
time: 291 us
  Pallas kernels  288 us (99%)
    pallas_call x1, Pallas kernels, on_square(): pl.pallas_call(functools.partial(exchange_kernel, banks, chunks, rows, ta...  263 us
    pallas_call x1, Pallas kernels, on_square(): pl.pallas_call(take_kernel, grid=(experts,), out_shape=tuple((jax.ShapeDt...  22.6 us
  transfers between devices with their start and end apart: 2, of which 1 were waited for; matrix products, arithmetic and copies ran while one was open for 0% of the time, Pallas kernels for 8%

profile of v2, /device:TPU:0, one launch (start us, length us, event | category | flops | bytes accessed | tf_op | source)
XLA Modules:
  0.0 291.2 jit_solution(12133870463839650559)
XLA Ops:
  0.6 262.9 %exchange.1 = (bf16[8,1024,2048]{2,1,0:T(8,128)(2,1)}, bf16[1,1024,512]{2,1,0:T(8,128)(2,1)}, bf16[1,1024,512]{2,1,0:T(8,128)(2,1)}, f32[8,1024]{1,0:T(8,128)}, bf16[64,2048]{1,0:T(8,128)(2,1)}) custom-call(f32[8,1024,512]{2,1,0:T(8,128)} %w_hbm.1, f32[8,1024,512]{2,1,0:T(8,128)} %a_hbm.1, f32[8]{0:T(128)} %mix_hbm.1, f32[8,512]{1,0:T(8,128)} %bitcast.3, ...), custom_call_target="tpu_custom_call" | custom-call | tf_op jit(solution)/shard_map/exchange/pallas_call | solution.py:333
  263.6 1.3 collective-permute-start
  264.8 0.8 collective-permute-start.1
  265.7 22.6 %take.1 = (bf16[8,1024,2048]{2,1,0:T(8,128)(2,1)}, f32[8,1024]{1,0:T(8,128)}, bf16[64,2048]{1,0:T(8,128)(2,1)}) custom-call(bf16[8,1024,2048]{2,1,0:T(8,128)(2,1)} %get-tuple-element.13.full, f32[8,1024]{1,0:T(8,128)} %get-tuple-element.14.scale, bf16[64,2048]{1,0:T(8,128)(2,1)} %get-tuple-element.15.router), custom_call_target="tpu_custom_call" | custom-call | bytes 67108864 | tf_op jit(solution)/shard_map/take/pallas_call | solution.py:378
  288.3 0.0 collective-permute-done.from_x
  288.3 0.3 collective-permute-done.1.from_y
  288.6 2.6 patch.1
Async XLA Ops:
  263.6 24.7 %collective-permute-start = (bf16[1,1024,512]{2,1,0:T(8,128)(2,1)}, bf16[1,1024,512]{2,1,0:T(8,128)(2,1)}, u32[]{:S(2)}, u32[]{:S(2)}) collective-permute-start(bf16[1,1024,512]{2,1,0:T(8,128)(2,1)} %get-tuple-element.11), channel_id=1, source_target_pairs={{0,1},{1,0},{2,3},{3,2},{4,5},{5,4},{6,7},{7,6},{8,9},{9,8},{10,11... | collective-permute-start | bytes 3145736 | tf_op jit(solution)/shard_map/ppermute | solution.py:376
  264.8 23.8 %collective-permute-start.1 = (bf16[1,1024,512]{2,1,0:T(8,128)(2,1)}, bf16[1,1024,512]{2,1,0:T(8,128)(2,1)}, u32[]{:S(2)}, u32[]{:S(2)}) collective-permute-start(bf16[1,1024,512]{2,1,0:T(8,128)(2,1)} %get-tuple-element.12), channel_id=1, source_target_pairs={{0,2},{1,3},{2,0},{3,1},{4,6},{5,7},{6,4},{7,5},{8,10},{9,11},{10,... | collective-permute-start | bytes 3145736 | tf_op jit(solution)/shard_map/ppermute | solution.py:377
